TPU v7x, 32 devices: a whole 2x2x4 slice. The times are simulated.
32 devices in a mesh: row: 4 (over x, core), col: 8 (over z, y).
Axes of the slice: x: 2, y: 2, z: 4, core: 2. Of those that a mesh axis runs over, the one named last changes fastest.
Arguments:
- picture_embedding_matrix: bfloat16 [2048, 1152], P(('row', 'col')), may hold values from -0.19921875 to 0.19921875
- caption_embedding_matrix: bfloat16 [2048, 1152], P(('row', 'col')), may hold values from -0.19921875 to 0.19921875
- sharpness_scale: float32 [1], replicated, may hold values from 4 to 12
- additive_shift: float32 [1], replicated, may hold values from -4 to -2
Outputs:
- grad_images: float32 [2048, 1152], P(('row', 'col'))
- grad_texts: float32 [2048, 1152], P(('row', 'col'))
- image_loss: float32 [2048], P(('row', 'col'))
All inputs are finite; a program needn't handle non-finite values.
Results may differ from a plain program's by a relative error of at most 0.0053.
Values may be sent and summed in bfloat16 or wider, within the bound.
A program may use at most 128 MiB of HBM per device.

v0:
```python
import jax
import jax.numpy as jnp
from jax import lax
from jax.sharding import PartitionSpec as P

EPS = 1e-06


def from_partner(shard, axis, apart):
    return lax.ppermute(shard, axis, [(i, i ^ 1 << apart) for i in range(lax.axis_size(axis))])


def normalize(feats):
    values = feats.astype(jnp.float32)
    inverse = lax.rsqrt(jnp.sum(values * values, axis=-1, keepdims=True) + EPS)
    return (values * inverse, inverse)


def back_norm(grad, unit, inverse):
    return inverse * (grad - unit * jnp.sum(unit * grad, axis=-1, keepdims=True))


def similarity_entry(
    picture_group,
    caption_group,
    picture_position,
    caption_position,
    sharpness_scale,
    additive_shift,
):
    similarity_matrix = (
        jnp.dot(picture_group, caption_group.T, preferred_element_type=jnp.float32)
        * sharpness_scale[0]
        + additive_shift[0]
    )
    match_sign = picture_position[:, None] == caption_position[None, :]
    label = jnp.where(match_sign, jnp.float32(1.0), jnp.float32(-1.0))
    sigmoid_loss = jnp.sum(jnp.log1p(jnp.exp(-label * similarity_matrix)), axis=1)
    logistic_weight = (
        sharpness_scale[0] * (jax.nn.sigmoid(similarity_matrix) - match_sign.astype(jnp.float32))
    ).astype(jnp.bfloat16)
    return (logistic_weight, sigmoid_loss)


def transpose_product(logistic_weight, picture_group):
    return lax.dot_general(
        logistic_weight, picture_group, (((0,), (0,)), ((), ())), preferred_element_type=jnp.float32
    )


def order_pair(mine, other, upper):
    lower_part = jnp.where(upper, other, mine)
    upper_part = jnp.where(upper, mine, other)
    return jnp.concatenate([lower_part, upper_part], axis=0)


def on_device(picture_embedding_matrix, caption_embedding_matrix, sharpness_scale, additive_shift):
    img_f, img_inv = normalize(picture_embedding_matrix)
    txt_f, txt_inv = normalize(caption_embedding_matrix)
    img_b = img_f.astype(jnp.bfloat16)
    caption_segment = txt_f.astype(jnp.bfloat16)
    sample_total = img_b.shape[0]
    n_row = lax.axis_size("row")
    n_col = lax.axis_size("col")
    row_at = lax.axis_index("row")
    col_at = lax.axis_index("col")
    low_bit = col_at % 2
    pair_col = col_at // 2
    levels = n_col.bit_length() - 1
    gathered = lax.all_gather(img_b, "row", axis=0, tiled=True)
    partner = from_partner(gathered, "col", 0)
    picture_group = order_pair(gathered, partner, low_bit == 1)
    img_local = jnp.arange(2 * n_row * sample_total, dtype=jnp.int32)
    img_half = img_local // (n_row * sample_total)
    img_row = img_local // sample_total % n_row
    picture_position = (
        img_row * n_col + 2 * pair_col + img_half
    ) * sample_total + img_local % sample_total
    caption_group = caption_segment
    for level in range(1, levels):
        level_bit = col_at // 2**level % 2
        other = from_partner(caption_group, "col", level)
        caption_group = order_pair(caption_group, other, level_bit == 1)
    text_local = jnp.arange(n_col // 2 * sample_total, dtype=jnp.int32)
    caption_position = (
        row_at * n_col + 2 * (text_local // sample_total) + low_bit
    ) * sample_total + text_local % sample_total
    logistic_weight, sigmoid_loss = similarity_entry(
        picture_group,
        caption_group,
        picture_position,
        caption_position,
        sharpness_scale,
        additive_shift,
    )
    partial_value = jnp.dot(logistic_weight, caption_group, preferred_element_type=jnp.float32)
    half_rows = n_row * sample_total
    upper = low_bit == 1
    keep_grad = jnp.where(upper, partial_value[half_rows:], partial_value[:half_rows])
    send_grad = jnp.where(upper, partial_value[:half_rows], partial_value[half_rows:])
    keep_loss = jnp.where(upper, sigmoid_loss[half_rows:], sigmoid_loss[:half_rows])
    send_loss = jnp.where(upper, sigmoid_loss[:half_rows], sigmoid_loss[half_rows:])
    got_grad, got_loss = from_partner((send_grad, send_loss), "col", 0)
    g_img, loss_own = (
        lax.psum_scatter(keep_grad + got_grad, "row", scatter_dimension=0, tiled=True),
        lax.psum_scatter(keep_loss + got_loss, "row", scatter_dimension=0, tiled=True),
    )
    text_part = transpose_product(logistic_weight, picture_group)
    for level in reversed(range(1, levels)):
        level_bit = col_at // 2**level % 2
        middle = text_part.shape[0] // 2
        keep_text = jnp.where(level_bit == 1, text_part[middle:], text_part[:middle])
        send_text = jnp.where(level_bit == 1, text_part[:middle], text_part[middle:])
        text_part = keep_text + from_partner(send_text, "col", level)
    return (back_norm(g_img, img_f, img_inv), back_norm(text_part, txt_f, txt_inv), loss_own)


def solution(mesh):
    placed = (P(("row", "col"), None), P(("row", "col"), None), P(), P())
    return jax.shard_map(
        on_device,
        mesh=mesh,
        in_specs=placed,
        out_specs=(P(("row", "col"), None), P(("row", "col"), None), P(("row", "col"))),
        check_vma=False,
    )
```

profile of v0, /device:TPU:0, one launch (start us, length us, event | category | flops | bytes accessed | tf_op | source)
XLA Modules:
  0.0 107.6 jit_solution(18370039871575645796)
XLA Ops:
  7.2 0.0 reduce-scatter.2.cloned.1.call-start
  7.2 1.0 fusion.24
  8.3 1.0 fusion.13
  9.3 3.1 %collective-permute-start.1 = (bf16[64,1152]{1,0:T(8,128)(2,1)S(1)}, bf16[64,1152]{1,0:T(8,128)(2,1)S(1)}, u32[]{:S(2)}, u32[]{:S(2)}) collective-permute-start(bf16[64,1152]{1,0:T(8,128)(2,1)S(1)} %fusion.13), channel_id=1, source_target_pairs={{0,2},{1,3},{2,0},{3,1},{4,6},{5,7},{6,4},{7,5},{8,10},{9,11},{10,... | collective-permute-start | bytes 442376 | tf_op jit(solution)/shard_map/ppermute | solution.py:10
  12.4 1.0 fusion.20
  13.5 1.0 fusion.16
  14.5 1.7 %collective-permute-done.1 = bf16[64,1152]{1,0:T(8,128)(2,1)S(1)} collective-permute-done((bf16[64,1152]{1,0:T(8,128)(2,1)S(1)}, bf16[64,1152]{1,0:T(8,128)(2,1)S(1)}, u32[]{:S(2)}, u32[]{:S(2)}) %collective-permute-start.1) | collective-permute-done | bytes 147488 | tf_op jit(solution)/shard_map/ppermute | solution.py:10
  16.2 1.0 broadcast_select_fusion.5
  17.3 2.8 %collective-permute-start.2 = (bf16[128,1152]{1,0:T(8,128)(2,1)S(1)}, bf16[128,1152]{1,0:T(8,128)(2,1)S(1)}, u32[]{:S(2)}, u32[]{:S(2)}) collective-permute-start(bf16[128,1152]{1,0:T(8,128)(2,1)S(1)} %pad_maximum_fusion.6), channel_id=1, source_target_pairs={{0,4},{1,5},{2,6},{3,7},{4,0},{5,1},{6,2},{7,3},{8,12},{9,13},{10,... | collective-permute-start | bytes 884744 | tf_op jit(solution)/shard_map/ppermute | solution.py:10
  20.1 7.5 %all_gather.3 = bf16[256,1152]{1,0:T(8,128)(2,1)S(1)} all-gather(bf16[64,1152]{1,0:T(8,128)(2,1)S(1)} %fusion.16), channel_id=1, replica_groups=mesh['row'=4,'col'=8] {'row'}, dimensions={0}, use_global_device_ids=true | all-gather | bytes 737280 | tf_op jit(solution)/shard_map/all_gather | solution.py:70
  27.7 1.5 %collective-permute-start = (bf16[256,1152]{1,0:T(8,128)(2,1)S(1)}, bf16[256,1152]{1,0:T(8,128)(2,1)S(1)}, u32[]{:S(2)}, u32[]{:S(2)}) collective-permute-start(bf16[256,1152]{1,0:T(8,128)(2,1)S(1)} %all_gather.3), channel_id=1, source_target_pairs={{0,1},{1,0},{2,3},{3,2},{4,5},{5,4},{6,7},{7,6},{8,9},{9,8},{10,11... | collective-permute-start | bytes 1769480 | tf_op jit(solution)/shard_map/ppermute | solution.py:10
  30.5 2.3 %collective-permute-done.2 = bf16[128,1152]{1,0:T(8,128)(2,1)S(1)} collective-permute-done((bf16[128,1152]{1,0:T(8,128)(2,1)S(1)}, bf16[128,1152]{1,0:T(8,128)(2,1)S(1)}, u32[]{:S(2)}, u32[]{:S(2)}) %collective-permute-start.2) | collective-permute-done | bytes 294944 | tf_op jit(solution)/shard_map/ppermute | solution.py:10
  32.8 0.1 broadcast_select_fusion.3
  32.9 10.3 %collective-permute-done = bf16[256,1152]{1,0:T(8,128)(2,1)S(1)} collective-permute-done((bf16[256,1152]{1,0:T(8,128)(2,1)S(1)}, bf16[256,1152]{1,0:T(8,128)(2,1)S(1)}, u32[]{:S(2)}, u32[]{:S(2)}) %collective-permute-start) | collective-permute-done | bytes 589856 | tf_op jit(solution)/shard_map/ppermute | solution.py:10
  43.2 0.1 broadcast_select_fusion.1
  43.4 0.8 fusion.9
  44.2 0.7 fusion.10
  44.8 0.1 slice_select_fusion
  45.0 1.6 %collective-permute-start.3 = (f32[256,1152]{1,0:T(8,128)S(1)}, f32[256,1152]{1,0:T(8,128)S(1)}, u32[]{:S(2)}, u32[]{:S(2)}) collective-permute-start(f32[256,1152]{1,0:T(8,128)S(1)} %slice_select_fusion), channel_id=1, source_target_pairs={{0,1},{1,0},{2,3},{3,2},{4,5},{5,4},{6,7},{7,6},{8,9},{9,8},{10,11... | collective-permute-start | bytes 3538952 | tf_op jit(solution)/shard_map/ppermute | solution.py:10
  46.6 0.6 fusion.1
  47.2 0.1 slice_select_fusion.1
  47.2 0.4 collective-permute-start.4
  47.7 24.7 %collective-permute-done.3 = f32[256,1152]{1,0:T(8,128)S(1)} collective-permute-done((f32[256,1152]{1,0:T(8,128)S(1)}, f32[256,1152]{1,0:T(8,128)S(1)}, u32[]{:S(2)}, u32[]{:S(2)}) %collective-permute-start.3) | collective-permute-done | bytes 1179680 | tf_op jit(solution)/shard_map/ppermute | solution.py:10
  72.4 1.2 %select_add_fusion = f32[256,1152]{1,0:T(8,128)} fusion(f32[256,1152]{1,0:T(8,128)S(1)} %collective-permute-done.3, f32[512,1152]{1,0:T(8,128)S(1)} %fusion.10, pred[]{:T(512)S(6)} %eq.38), kind=kLoop, calls=%fused_computation.3 | loop fusion | flops 589824 | bytes 4718593 | tf_op jit(solution)/shard_map/add | solution.py:105
  73.6 0.0 reduce-scatter.2.cloned.1.call-update
  73.6 0.0 copy-start.2
  73.6 0.0 copy-start
  73.6 1.7 %collective-permute-done.4 = f32[128,1152]{1,0:T(8,128)S(1)} collective-permute-done((f32[128,1152]{1,0:T(8,128)S(1)}, f32[128,1152]{1,0:T(8,128)S(1)}, u32[]{:S(2)}, u32[]{:S(2)}) %collective-permute-start.4) | collective-permute-done | bytes 589856 | tf_op jit(solution)/shard_map/ppermute | solution.py:10
  75.3 0.1 select_add_fusion.1
  75.4 0.0 copy-start.1
  75.4 0.1 collective-permute-start.5
  75.5 1.4 %collective-permute-start.6 = (f32[256]{0:T(256)S(1)}, f32[256]{0:T(256)S(1)}, u32[]{:S(2)}, u32[]{:S(2)}) collective-permute-start(f32[256]{0:T(256)S(1)} %broadcast_select_fusion.6), channel_id=1, source_target_pairs={{0,1},{1,0},{2,3},{3,2},{4,5},{5,4},{6,7},{7,6},{8,9},{9,8},{10,11... | collective-permute-start | bytes 3080 | tf_op jit(solution)/shard_map/ppermute | solution.py:10
  77.0 0.0 copy-done.2
  77.0 0.6 dynamic-slice
  78.2 1.0 collective-permute-done.6
  79.2 5.9 %all-reduce = f32[256]{0:T(256)S(1)} all-reduce(f32[256]{0:T(256)S(1)} %select_add_fusion.3), channel_id=3, replica_groups=mesh['row'=4,'col'=8] {'row'}, use_global_device_ids=true, to_apply=%region_6.7.clone | all-reduce | flops 256 | bytes 2048
  85.1 0.6 dynamic-slice.1
  85.7 0.0 collective-permute-done.5
  85.7 0.0 copy-done
  85.7 0.2 fusion.21
  85.9 0.8 fusion.23
  86.7 11.0 %reduce-scatter.2.cloned.1.call-done = f32[64,1152]{1,0:T(8,128)} async-done(((f32[256,1152]{1,0:T(8,128)}), f32[64,1152]{1,0:T(8,128)}) %reduce-scatter.2.cloned.1.call-update) | async-done | bytes 294928 | tf_op jit(solution)/shard_map/reduce_scatter | solution.py:105
  97.8 0.0 copy-done.1
  97.8 1.2 %fusion.17 = f32[64]{0:T(128)S(1)} fusion(f32[64,1152]{1,0:T(8,128)} %reduce-scatter.2.cloned.1.call-done, bf16[64,1152]{1,0:T(8,128)(2,1)S(1)} %copy-done.1, f32[64]{0:T(128)S(1)} %add_rsqrt_fusion.1), kind=kLoop, calls=%fused_computation.32 | loop fusion | flops 294848 | bytes 442880 | tf_op jit(solution)/shard_map/reduce_sum | solution.py:20
  98.9 1.8 %fusion.19 = f32[64,1152]{1,0:T(8,128)} fusion(f32[64,1152]{1,0:T(8,128)} %reduce-scatter.2.cloned.1.call-done, bf16[64,1152]{1,0:T(8,128)(2,1)S(1)} %copy-done.1, f32[64]{0:T(128)S(1)} %fusion.17, f32[64]{0:T(128)S(1)} %add_rsqrt_fusion.1), kind=kLoop, calls=%fused_computation.34 | loop fusion | flops 368640 | bytes 737792 | tf_op jit(solution)/shard_map/mul | solution.py:20
  (8 shorter events, 0.1 us)
Async XLA Ops:
  7.2 90.6 %reduce-scatter.2.cloned.1.call-start = ((), (), s32[]{:S(2)}) async-start(), calls=%async_computation.1 | async-start | bytes 1474560 | tf_op jit(solution)/shard_map/reduce_scatter | solution.py:105
  9.3 7.0 %collective-permute-start.1 = (bf16[64,1152]{1,0:T(8,128)(2,1)S(1)}, bf16[64,1152]{1,0:T(8,128)(2,1)S(1)}, u32[]{:S(2)}, u32[]{:S(2)}) collective-permute-start(bf16[64,1152]{1,0:T(8,128)(2,1)S(1)} %fusion.13), channel_id=1, source_target_pairs={{0,2},{1,3},{2,0},{3,1},{4,6},{5,7},{6,4},{7,5},{8,10},{9,11},{10,... | collective-permute-start | bytes 442376 | tf_op jit(solution)/shard_map/ppermute | solution.py:10
  17.3 15.5 %collective-permute-start.2 = (bf16[128,1152]{1,0:T(8,128)(2,1)S(1)}, bf16[128,1152]{1,0:T(8,128)(2,1)S(1)}, u32[]{:S(2)}, u32[]{:S(2)}) collective-permute-start(bf16[128,1152]{1,0:T(8,128)(2,1)S(1)} %pad_maximum_fusion.6), channel_id=1, source_target_pairs={{0,4},{1,5},{2,6},{3,7},{4,0},{5,1},{6,2},{7,3},{8,12},{9,13},{10,... | collective-permute-start | bytes 884744 | tf_op jit(solution)/shard_map/ppermute | solution.py:10
  27.7 15.6 %collective-permute-start = (bf16[256,1152]{1,0:T(8,128)(2,1)S(1)}, bf16[256,1152]{1,0:T(8,128)(2,1)S(1)}, u32[]{:S(2)}, u32[]{:S(2)}) collective-permute-start(bf16[256,1152]{1,0:T(8,128)(2,1)S(1)} %all_gather.3), channel_id=1, source_target_pairs={{0,1},{1,0},{2,3},{3,2},{4,5},{5,4},{6,7},{7,6},{8,9},{9,8},{10,11... | collective-permute-start | bytes 1769480 | tf_op jit(solution)/shard_map/ppermute | solution.py:10
  45.0 27.4 %collective-permute-start.3 = (f32[256,1152]{1,0:T(8,128)S(1)}, f32[256,1152]{1,0:T(8,128)S(1)}, u32[]{:S(2)}, u32[]{:S(2)}) collective-permute-start(f32[256,1152]{1,0:T(8,128)S(1)} %slice_select_fusion), channel_id=1, source_target_pairs={{0,1},{1,0},{2,3},{3,2},{4,5},{5,4},{6,7},{7,6},{8,9},{9,8},{10,11... | collective-permute-start | bytes 3538952 | tf_op jit(solution)/shard_map/ppermute | solution.py:10
  47.2 28.0 %collective-permute-start.4 = (f32[128,1152]{1,0:T(8,128)S(1)}, f32[128,1152]{1,0:T(8,128)S(1)}, u32[]{:S(2)}, u32[]{:S(2)}) collective-permute-start(f32[128,1152]{1,0:T(8,128)S(1)} %slice_select_fusion.1), channel_id=1, source_target_pairs={{0,4},{1,5},{2,6},{3,7},{4,0},{5,1},{6,2},{7,3},{8,12},{9,13},{10,... | collective-permute-start | bytes 1769480 | tf_op jit(solution)/shard_map/ppermute | solution.py:10
  73.6 3.4 %copy-start.2 = (u32[32]{0:T(128)S(1)}, u32[32]{0:T(128)}, u32[]{:S(2)}) copy-start(u32[32]{0:T(128)} %constant.147) | copy-start | bytes 388
  73.6 12.1 %copy-start = (bf16[64,1152]{1,0:T(8,128)(2,1)S(1)}, bf16[64,1152]{1,0:T(8,128)(2,1)}, u32[]{:S(2)}) copy-start(bf16[64,1152]{1,0:T(8,128)(2,1)} %param.5) | copy-start | bytes 442372
  75.4 22.3 %copy-start.1 = (bf16[64,1152]{1,0:T(8,128)(2,1)S(1)}, bf16[64,1152]{1,0:T(8,128)(2,1)}, u32[]{:S(2)}) copy-start(bf16[64,1152]{1,0:T(8,128)(2,1)} %param.4) | copy-start | bytes 442372
  75.4 10.2 %collective-permute-start.5 = (f32[64,1152]{1,0:T(8,128)S(1)}, f32[64,1152]{1,0:T(8,128)S(1)}, u32[]{:S(2)}, u32[]{:S(2)}) collective-permute-start(f32[64,1152]{1,0:T(8,128)S(1)} %slice_select_fusion.2), channel_id=1, source_target_pairs={{0,2},{1,3},{2,0},{3,1},{4,6},{5,7},{6,4},{7,5},{8,10},{9,11},{10,... | collective-permute-start | bytes 884744 | tf_op jit(solution)/shard_map/ppermute | solution.py:10
  75.5 3.6 %collective-permute-start.6 = (f32[256]{0:T(256)S(1)}, f32[256]{0:T(256)S(1)}, u32[]{:S(2)}, u32[]{:S(2)}) collective-permute-start(f32[256]{0:T(256)S(1)} %broadcast_select_fusion.6), channel_id=1, source_target_pairs={{0,1},{1,0},{2,3},{3,2},{4,5},{5,4},{6,7},{7,6},{8,9},{9,8},{10,11... | collective-permute-start | bytes 3080 | tf_op jit(solution)/shard_map/ppermute | solution.py:10
Sparse Core Ops, SparseCore 0:
  73.7 23.9 reduce-scatter.1
where the time goes:
time: 108 us
  waiting for transfers between devices  52.8 us (49%)
  between operations  16.2 us (15%)
  blocking collectives  13.4 us (12%)
  starting transfers between devices  11 us (10%)
  other arithmetic  10.9 us (10%)
  matrix products  2.09 us (2%)
  local copies, waits for them, and re-layouts  1.19 us (1%)
    ppermute x7, waiting for transfers between devices, from_partner(): lax.ppermute(shard, axis, [(i, i ^ 1 << apart) for i in range(lax.axis_si...  41.8 us
    reduce_scatter x1, waiting for transfers between devices, on_device(): lax.psum_scatter(keep_grad + got_grad, 'row', scatter_dimension=0, tiled=...  11 us
    ppermute x7, starting transfers between devices, from_partner(): lax.ppermute(shard, axis, [(i, i ^ 1 << apart) for i in range(lax.axis_si...  10.9 us
    all_gather x1, blocking collectives, on_device(): gathered = lax.all_gather(img_b, 'row', axis=0, tiled=True)  7.51 us
    unnamed x1, blocking collectives  5.92 us
    mul x2, other arithmetic, back_norm(): inverse * (grad - unit * jnp.sum(unit * grad, axis=-1, keepdims=True))  2.64 us
  transfers between devices with their start and end apart: 8, of which 7 were waited for; matrix products, arithmetic and copies ran while one was open for 6% of the time, Pallas kernels for 0%

commit v1 on v0

v1 whole, which is shorter than its diff:
```python
import functools

import jax
import jax.numpy as jnp
from jax import lax
from jax.experimental import pallas as pl
from jax.experimental.pallas import tpu as pltpu
from jax.sharding import PartitionSpec as P

EPS = 1e-06
MESH = pl.DeviceIdType.MESH
PIECES = 2
TILE = 256


def bits_of(n):
    return n.bit_length() - 1


def groups(n_row, n_col):
    row_bits, col_bits = bits_of(n_row), bits_of(n_col)
    take = min(max((row_bits + col_bits + 1) // 2 - row_bits, 0), col_bits)
    choice = [b for b in range(1, col_bits)] + [0] * (col_bits > 0)
    mine, rest = choice[:take], choice[take:]
    images = [("col", b) for b in sorted(mine, reverse=True)]
    images += [("row", b) for b in reversed(range(row_bits))]
    texts = [("col", b) for b in sorted(rest, reverse=True)]
    return images, texts


def flip(index, bit):
    step = 2**bit
    return index + step * (1 - 2 * lax.rem(lax.div(index, step), 2))


def peer_of(dims, mask):
    at = {"row": lax.axis_index("row"), "col": lax.axis_index("col")}
    for j, (axis, bit) in enumerate(dims):
        if mask >> j & 1:
            at[axis] = flip(at[axis], bit)
    return (at["row"], at["col"])


def top(slot):
    return slot.bit_length() - 1


def inverse_norm(values):
    return lax.rsqrt(jnp.sum(values * values, axis=-1, keepdims=True) + EPS)


def tiles(count, body):
    if count <= 4:
        for t in range(count):
            body(t)
    else:
        lax.fori_loop(0, count, lambda t, _: (body(t), 0)[1], 0)


def kernel(
    dims,
    own_img,
    own_txt,
    scale_ref,
    shift_ref,
    gi_ref,
    gt_ref,
    loss_ref,
    img_raw,
    txt_raw,
    img_n,
    txt_n,
    coef,
    acc_img,
    acc_txt,
    out_img,
    out_txt,
    in_img,
    in_txt,
    loss_sum,
    loss_out,
    loss_in,
    gs_img,
    gr_img,
    gs_txt,
    gr_txt,
    ss_img,
    sr_img,
    ss_txt,
    sr_txt,
    ls,
    lr,
):
    rows, _ = own_img.shape
    part = rows // PIECES
    size = {"i": 2 ** len(dims["i"]), "t": 2 ** len(dims["t"])}
    own = {"i": own_img, "t": own_txt}
    raw = {"i": img_raw, "t": txt_raw}
    unit = {"i": img_n, "t": txt_n}
    acc = {"i": acc_img, "t": acc_txt}
    out = {"i": out_img, "t": out_txt}
    into = {"i": in_img, "t": in_txt}
    g_sems = {"i": (gs_img, gr_img), "t": (gs_txt, gr_txt)}
    s_sems = {"i": (ss_img, sr_img), "t": (ss_txt, sr_txt)}
    sent = []

    peers = [peer_of(dims["i"], m) for m in range(1, size["i"])]
    peers += [peer_of(dims["t"], 2**j) for j in range(len(dims["t"]))]
    barrier = pltpu.get_barrier_semaphore()
    for peer in peers:
        pl.semaphore_signal(barrier, inc=1, device_id=peer, device_id_type=MESH)
    pl.semaphore_wait(barrier, len(peers))

    gather = {}

    def spread(g, slot, j, p):
        to = slot | 1 << j
        piece = pl.ds(p * part, part)
        source = own[g].at[piece] if slot == 0 else raw[g].at[slot, piece]
        copy = pltpu.make_async_remote_copy(
            src_ref=source,
            dst_ref=raw[g].at[to, piece],
            send_sem=g_sems[g][0].at[to, p],
            recv_sem=g_sems[g][1].at[to, p],
            device_id=peer_of(dims[g], 1 << j),
            device_id_type=MESH,
        )
        copy.start()
        gather[g, to, p] = copy
        sent.append(copy)

    for p in range(PIECES):
        for j in range(max(len(dims["i"]), len(dims["t"]))):
            for g in ("t", "i"):
                if j < len(dims[g]):
                    spread(g, 0, j, p)

    def normalize(g, slot):
        values = (own[g][...] if slot == 0 else raw[g][slot]).astype(jnp.float32)
        unit[g][slot * rows : (slot + 1) * rows, :] = (values * inverse_norm(values)).astype(
            jnp.bfloat16
        )

    normalize("i", 0)
    normalize("t", 0)
    levels = max(len(dims["i"]), len(dims["t"]))
    for level in range(1, levels + 1):
        slots = [
            (g, s)
            for s in reversed(range(1, max(size.values())))
            for g in ("i", "t")
            if s < size[g] and s.bit_count() == level
        ]
        for p in range(PIECES):
            for g, s in slots:
                gather[g, s, p].wait_recv()
                for j in range(top(s) + 1, len(dims[g])):
                    spread(g, s, j, p)
                if p == PIECES - 1:
                    normalize(g, s)

    scale, shift = scale_ref[0], shift_ref[0]
    n_img, n_txt = size["i"] * rows, size["t"] * rows
    t_img, t_txt = min(TILE, n_img), min(TILE, n_txt)
    loss_sum[...] = jnp.zeros_like(loss_sum)

    def logits(t):
        if isinstance(t, int):
            at_txt, at_img = t // (n_img // t_img) * t_txt, t % (n_img // t_img) * t_img
        else:
            at_txt = pl.multiple_of(lax.div(t, n_img // t_img) * t_txt, t_txt)
            at_img = pl.multiple_of(lax.rem(t, n_img // t_img) * t_img, t_img)
        here_txt, here_img = pl.ds(at_txt, t_txt), pl.ds(at_img, t_img)
        value = lax.dot_general(
            txt_n[here_txt, :],
            img_n[here_img, :],
            (((1,), (1,)), ((), ())),
            preferred_element_type=jnp.float32,
        )
        value = value * scale + shift
        weight = scale
        if not isinstance(t, int) or t == 0:
            a = lax.broadcasted_iota(jnp.int32, value.shape, 0) + at_txt
            b = lax.broadcasted_iota(jnp.int32, value.shape, 1) + at_img
            match = (a == b) & (a < rows)
            value = jnp.where(match, -value, value)
            weight = jnp.where(match, -scale, scale)
        e = jnp.exp(value)
        loss_sum[:, here_img] += jnp.sum(jnp.log1p(e), axis=0, keepdims=True)
        coef[here_txt, here_img] = (weight * (e / (1.0 + e))).astype(jnp.bfloat16)

    tiles((n_txt // t_txt) * (n_img // t_img), logits)

    losses = []
    for s in range(1, size["i"]):
        loss_out[s] = loss_sum[:, s * rows : (s + 1) * rows]
        copy = pltpu.make_async_remote_copy(
            src_ref=loss_out.at[s],
            dst_ref=loss_in.at[s],
            send_sem=ls.at[s],
            recv_sem=lr.at[s],
            device_id=peer_of(dims["i"], s),
            device_id_type=MESH,
        )
        copy.start()
        losses.append(copy)
        sent.append(copy)

    scatter = {}

    def pass_on(g, s, p):
        piece = pl.ds(p * part, part)
        copy = pltpu.make_async_remote_copy(
            src_ref=out[g].at[s, piece],
            dst_ref=into[g].at[s, piece],
            send_sem=s_sems[g][0].at[s, p],
            recv_sem=s_sems[g][1].at[s, p],
            device_id=peer_of(dims[g], 1 << top(s)),
            device_id_type=MESH,
        )
        copy.start()
        scatter[g, s, p] = copy
        sent.append(copy)

    def product(g, first, count):
        here = pl.ds(first * rows, count * rows)
        if not isinstance(first, int):
            here = pl.ds(pl.multiple_of(first * rows, count * rows), count * rows)
        if g == "t":
            return jnp.dot(coef[here, :], img_n[...], preferred_element_type=jnp.float32)
        return lax.dot_general(
            coef[:, here], txt_n[...], (((0,), (0,)), ((), ())), preferred_element_type=jnp.float32
        )

    def grads(g, upper):
        half = size[g] // 2
        base = half if upper else 0
        step = min(half, TILE // rows)

        def body(t):
            first = base + t * step
            value = product(g, first, step)
            if upper:
                out[g][pl.ds(first, step)] = value.reshape(step, rows, -1).astype(jnp.bfloat16)
            else:
                acc[g][pl.ds(first, step)] = value.reshape(step, rows, -1)

        tiles(half // step, body)
        if upper:
            for s in reversed(range(half, size[g])):
                for p in range(PIECES):
                    pass_on(g, s, p)

    grads("t", True)
    grads("i", True)
    grads("i", False)
    grads("t", False)

    def total(g, k, p):
        piece = pl.ds(p * part, part)
        value = acc[g][k, piece]
        for j in reversed(range(top(k) + 1 if k else 0, len(dims[g]))):
            scatter[g, k | 1 << j, p].wait_recv()
            value = value + into[g][k | 1 << j, piece].astype(jnp.float32)
        return value

    order = sorted(
        [(k.bit_length() - len(dims[g]), g, k) for g in ("i", "t") for k in range(1, size[g] // 2)],
        key=lambda item: (-item[0], item[1] != "i", -item[2]),
    )
    for _, g, k in order:
        for p in range(PIECES):
            out[g][k, pl.ds(p * part, part)] = total(g, k, p).astype(jnp.bfloat16)
            pass_on(g, k, p)

    value = loss_sum[:, :rows]
    for s, copy in enumerate(losses, 1):
        copy.wait_recv()
        value = value + loss_in[s]
    loss_ref[...] = value

    for g, result in (("i", gi_ref), ("t", gt_ref)):
        for p in range(PIECES):
            piece = pl.ds(p * part, part)
            grad = total(g, 0, p)
            values = own[g][piece].astype(jnp.float32)
            inverse = inverse_norm(values)
            unit_row = values * inverse
            along = jnp.sum(unit_row * grad, axis=-1, keepdims=True)
            result[piece, :] = inverse * (grad - unit_row * along)

    for copy in sent:
        copy.wait_send()


def on_device(n_row, n_col, images, texts, scale, shift):
    rows, width = images.shape
    dims = dict(zip("it", groups(n_row, n_col)))
    a, b = 2 ** len(dims["i"]), 2 ** len(dims["t"])
    vmem = pl.BlockSpec(memory_space=pltpu.VMEM)
    smem = pl.BlockSpec(memory_space=pltpu.SMEM)
    f32, bf16 = jnp.float32, jnp.bfloat16
    gi, gt, loss = pl.pallas_call(
        functools.partial(kernel, dims),
        out_shape=(
            jax.ShapeDtypeStruct((rows, width), f32),
            jax.ShapeDtypeStruct((rows, width), f32),
            jax.ShapeDtypeStruct((1, rows), f32),
        ),
        in_specs=[vmem, vmem, smem, smem],
        out_specs=(vmem, vmem, vmem),
        scratch_shapes=[
            pltpu.VMEM((a, rows, width), bf16),
            pltpu.VMEM((b, rows, width), bf16),
            pltpu.VMEM((a * rows, width), bf16),
            pltpu.VMEM((b * rows, width), bf16),
            pltpu.VMEM((b * rows, a * rows), bf16),
            pltpu.VMEM((a // 2, rows, width), f32),
            pltpu.VMEM((b // 2, rows, width), f32),
            pltpu.VMEM((a, rows, width), bf16),
            pltpu.VMEM((b, rows, width), bf16),
            pltpu.VMEM((a, rows, width), bf16),
            pltpu.VMEM((b, rows, width), bf16),
            pltpu.VMEM((1, a * rows), f32),
            pltpu.VMEM((a, 1, rows), f32),
            pltpu.VMEM((a, 1, rows), f32),
        ]
        + [pltpu.SemaphoreType.DMA((n, PIECES)) for n in (a, a, b, b, a, a, b, b)]
        + [pltpu.SemaphoreType.DMA((a,)), pltpu.SemaphoreType.DMA((a,))],
        compiler_params=pltpu.CompilerParams(collective_id=0, has_side_effects=True),
    )(images, texts, scale, shift)
    return gi, gt, loss.reshape(rows)


def solution(mesh):
    placed = (P(("row", "col"), None), P(("row", "col"), None), P(), P())
    return jax.shard_map(
        functools.partial(on_device, mesh.shape["row"], mesh.shape["col"]),
        mesh=mesh,
        in_specs=placed,
        out_specs=(P(("row", "col"), None), P(("row", "col"), None), P(("row", "col"))),
        check_vma=False,
    )
```

time: 108 us -> 40.2 us (0.37)
  waiting for transfers between devices: 52.8 us -> 0 us
  Pallas kernels: 0 us -> 35.1 us
  between operations: 16.2 us -> 1.94 us
  blocking collectives: 13.4 us -> 0 us
  starting transfers between devices: 11 us -> 0 us
  other arithmetic: 10.9 us -> 0 us
  matrix products: 2.09 us -> 0 us
  local copies, waits for them, and re-layouts: 1.19 us -> 2.97 us
    ppermute x7 -> x0, waiting for transfers between devices: 41.8 us -> none  [from_partner(): lax.ppermute(shard, axis, [(i, i ^ 1 << apart) for i in range(lax.axis_si...]
    pallas_call x0 -> x1, Pallas kernels: none -> 35.1 us  [on_device(): pl.pallas_call(functools.partial(kernel, dims), out_shape=(jax.ShapeDtype...]
    reduce_scatter x1 -> x0, waiting for transfers between devices: 11 us -> none  [on_device(): lax.psum_scatter(keep_grad + got_grad, 'row', scatter_dimension=0, tiled=...]
    ppermute x7 -> x0, starting transfers between devices: 10.9 us -> none  [from_partner(): lax.ppermute(shard, axis, [(i, i ^ 1 << apart) for i in range(lax.axis_si...]
    all_gather x1 -> x0, blocking collectives: 7.51 us -> none  [on_device(): gathered = lax.all_gather(img_b, 'row', axis=0, tiled=True)]
    unnamed x1 -> x0, blocking collectives: 5.92 us -> none
    reduce_sum x4 -> x0, other arithmetic: 3.45 us -> none  [the longest x2 2.08 us: normalize(): inverse = lax.rsqrt(jnp.sum(values * values, axis=-1, keepdims=True) + EPS)]
    mul x2 -> x0, other arithmetic: 2.64 us -> none  [back_norm(): inverse * (grad - unit * jnp.sum(unit * grad, axis=-1, keepdims=True))]
  transfers between devices with their start and end apart: 8 -> 0, of which waited for: 7 -> 0; matrix products, arithmetic and copies ran while one was open for 6% -> 0% of each run, Pallas kernels for 0% -> 0%
where the time goes in v1:
time: 40.2 us; the launch traced here: 40.1 us
  Pallas kernels  35.1 us (87%)
  local copies, waits for them, and re-layouts  2.97 us (7%)
  between operations  1.94 us (5%)
    pallas_call x1, Pallas kernels, on_device(): pl.pallas_call(functools.partial(kernel, dims), out_shape=(jax.ShapeDtype...  35.1 us
    unnamed x7, local copies, waits for them, and re-layouts  2.97 us

profile of v1, /device:TPU:0, one launch (start us, length us, event | category | flops | bytes accessed | tf_op | source)
XLA Modules:
  0.0 40.1 jit_solution(631591700252555479)
XLA Ops:
  1.9 35.1 %shard_map.67 = (f32[64,1152]{1,0:T(8,128)}, f32[64,1152]{1,0:T(8,128)}, f32[1,64]{1,0:T(1,128)}) custom-call(bf16[64,1152]{1,0:T(8,128)(2,1)} %own_img.1, bf16[64,1152]{1,0:T(8,128)(2,1)} %own_txt.1, f32[1]{0:T(128)S(6)} %copy.10.scale_ref, f32[1]{0:T(128)S(6)} %copy.11.shift_ref), custom_call_target="tpu_custom_call" | custom-call | tf_op jit(solution)/shard_map/pallas_call | solution.py:303
  37.1 0.0 copy-start
  37.1 1.7 %copy.12 = f32[64,1152]{1,0:T(8,128)} copy(f32[64,1152]{1,0:T(8,128)} %get-tuple-element.12) | data formatting | bytes 589824
  38.8 0.0 copy-done
  38.8 0.0 copy-start.1
  38.8 0.7 %copy.13 = f32[64,1152]{1,0:T(8,128)} copy(f32[64,1152]{1,0:T(8,128)S(1)} %copy-done) | data formatting | bytes 589824
  39.5 0.0 copy-done.1
  39.5 0.5 %copy.14 = f32[64]{0:T(128)} copy(f32[64]{0:T(128)S(1)} %bitcast.1) | data formatting | bytes 512
Async XLA Ops:
  37.1 1.8 %copy-start = (f32[64,1152]{1,0:T(8,128)S(1)}, f32[64,1152]{1,0:T(8,128)}, u32[]{:S(2)}) copy-start(f32[64,1152]{1,0:T(8,128)} %get-tuple-element.13) | copy-start | bytes 884740
  38.8 0.7 %copy-start.1 = (f32[1,64]{1,0:T(1,128)S(1)}, f32[1,64]{1,0:T(1,128)}, u32[]{:S(2)}) copy-start(f32[1,64]{1,0:T(1,128)} %get-tuple-element.8) | copy-start | bytes 772

commit v2 on v1

--- a/solution.py
+++ b/solution.py
@@ -59,13 +59,16 @@
 
 def kernel(
     dims,
-    own_img,
-    own_txt,
+    img_hbm,
+    txt_hbm,
     scale_ref,
     shift_ref,
     gi_ref,
     gt_ref,
     loss_ref,
+    own_img,
+    own_txt,
+    load,
     img_raw,
     txt_raw,
     img_n,
@@ -91,7 +94,7 @@
     ls,
     lr,
 ):
-    rows, _ = own_img.shape
+    rows, _ = img_hbm.shape
     part = rows // PIECES
     size = {"i": 2 ** len(dims["i"]), "t": 2 ** len(dims["t"])}
     own = {"i": own_img, "t": own_txt}
@@ -109,6 +112,19 @@
     barrier = pltpu.get_barrier_semaphore()
     for peer in peers:
         pl.semaphore_signal(barrier, inc=1, device_id=peer, device_id_type=MESH)
+    loads = [
+        pltpu.make_async_copy(source, target, load.at[n])
+        for n, (source, target) in enumerate(
+            [
+                (txt_hbm, own_txt),
+                (img_hbm, own_img),
+            ]
+        )
+    ]
+    for copy in loads:
+        copy.start()
+    for copy in loads:
+        copy.wait()
     pl.semaphore_wait(barrier, len(peers))
 
     gather = {}
@@ -131,7 +147,7 @@
 
     for p in range(PIECES):
         for j in range(max(len(dims["i"]), len(dims["t"]))):
-            for g in ("t", "i"):
+            for g in ("i", "t"):
                 if j < len(dims[g]):
                     spread(g, 0, j, p)
 
@@ -293,23 +309,36 @@
         copy.wait_send()
 
 
+def hand_out(gi_from, gt_from, loss_from, gi_ref, gt_ref, loss_ref, sems):
+    pairs = ((gi_from, gi_ref), (gt_from, gt_ref), (loss_from, loss_ref))
+    copies = [pltpu.make_async_copy(a, b, sems.at[n]) for n, (a, b) in enumerate(pairs)]
+    for copy in copies:
+        copy.start()
+    for copy in copies:
+        copy.wait()
+
+
 def on_device(n_row, n_col, images, texts, scale, shift):
     rows, width = images.shape
     dims = dict(zip("it", groups(n_row, n_col)))
     a, b = 2 ** len(dims["i"]), 2 ** len(dims["t"])
     vmem = pl.BlockSpec(memory_space=pltpu.VMEM)
     smem = pl.BlockSpec(memory_space=pltpu.SMEM)
+    hbm = pl.BlockSpec(memory_space=pl.ANY)
     f32, bf16 = jnp.float32, jnp.bfloat16
-    gi, gt, loss = pl.pallas_call(
+    sums = pl.pallas_call(
         functools.partial(kernel, dims),
         out_shape=(
-            jax.ShapeDtypeStruct((rows, width), f32),
-            jax.ShapeDtypeStruct((rows, width), f32),
-            jax.ShapeDtypeStruct((1, rows), f32),
+            pltpu.VMEM((rows, width), f32),
+            pltpu.VMEM((rows, width), f32),
+            pltpu.VMEM((1, rows), f32),
         ),
-        in_specs=[vmem, vmem, smem, smem],
+        in_specs=[hbm, hbm, smem, smem],
         out_specs=(vmem, vmem, vmem),
         scratch_shapes=[
+            pltpu.VMEM((rows, width), bf16),
+            pltpu.VMEM((rows, width), bf16),
+            pltpu.SemaphoreType.DMA((2,)),
             pltpu.VMEM((a, rows, width), bf16),
             pltpu.VMEM((b, rows, width), bf16),
             pltpu.VMEM((a * rows, width), bf16),
@@ -328,7 +357,18 @@
         + [pltpu.SemaphoreType.DMA((n, PIECES)) for n in (a, a, b, b, a, a, b, b)]
         + [pltpu.SemaphoreType.DMA((a,)), pltpu.SemaphoreType.DMA((a,))],
         compiler_params=pltpu.CompilerParams(collective_id=0, has_side_effects=True),
-    )(images, texts, scale, shift)
+    )(*[pltpu.with_memory_space_constraint(x, pltpu.HBM) for x in (images, texts)], scale, shift)
+    gi, gt, loss = pl.pallas_call(
+        hand_out,
+        out_shape=(
+            jax.ShapeDtypeStruct((rows, width), f32),
+            jax.ShapeDtypeStruct((rows, width), f32),
+            jax.ShapeDtypeStruct((1, rows), f32),
+        ),
+        in_specs=[hbm] * 3,
+        out_specs=(hbm, hbm, hbm),
+        scratch_shapes=[pltpu.SemaphoreType.DMA((3,))],
+    )(*[pltpu.with_memory_space_constraint(x, pltpu.VMEM) for x in sums])
     return gi, gt, loss.reshape(rows)
 
 

time: 40.2 us -> 34.9 us (0.87)
  local copies, waits for them, and re-layouts: 2.97 us -> 0 us
  Pallas kernels: 35.1 us -> 32.8 us
    unnamed x7 -> x0, local copies, waits for them, and re-layouts: 2.97 us -> none
    pallas_call x1 -> x2, Pallas kernels: 35.1 us -> 32.8 us  [the longest x1 32 us: on_device(): pl.pallas_call(functools.partial(kernel, dims), out_shape=(pltpu.VMEM((ro...]
where the time goes in v2:
time: 34.9 us; the launch traced here: 34.7 us
  Pallas kernels  32.8 us (94%)
  between operations  1.93 us (6%)
    pallas_call x1, Pallas kernels, on_device(): pl.pallas_call(functools.partial(kernel, dims), out_shape=(pltpu.VMEM((ro...  32 us
    pallas_call x1, Pallas kernels, on_device(): pl.pallas_call(hand_out, out_shape=(jax.ShapeDtypeStruct((rows, width), f...  0.84 us

profile of v2, /device:TPU:0, one launch (start us, length us, event | category | flops | bytes accessed | tf_op | source)
XLA Modules:
  0.0 34.7 jit_solution(2315137283548969225)
XLA Ops:
  1.9 32.0 %shard_map.67 = (f32[64,1152]{1,0:T(8,128)S(1)}, f32[64,1152]{1,0:T(8,128)S(1)}, f32[1,64]{1,0:T(1,128)S(1)}) custom-call(bf16[64,1152]{1,0:T(8,128)(2,1)} %img_hbm.1, bf16[64,1152]{1,0:T(8,128)(2,1)} %txt_hbm.1, f32[1]{0:T(128)S(6)} %copy.7.scale_ref, f32[1]{0:T(128)S(6)} %copy.8.shift_ref), custom_call_target="tpu_custom_call" | custom-call | tf_op jit(solution)/shard_map/pallas_call | solution.py:329
  33.9 0.8 %shard_map.68 = (f32[64,1152]{1,0:T(8,128)}, f32[64,1152]{1,0:T(8,128)}, f32[1,64]{1,0:T(1,128)}) custom-call(f32[64,1152]{1,0:T(8,128)S(1)} %get-tuple-element.9.gi_from, f32[64,1152]{1,0:T(8,128)S(1)} %get-tuple-element.10.gt_from, f32[1,64]{1,0:T(1,128)S(1)} %get-tuple-element.11.loss_from), custom_call_target="tpu_custom_call" | custom-call | tf_op jit(solution)/shard_map/pallas_call | solution.py:361

commit v3 on v2

--- a/solution.py
+++ b/solution.py
@@ -289,12 +289,6 @@
             out[g][k, pl.ds(p * part, part)] = total(g, k, p).astype(jnp.bfloat16)
             pass_on(g, k, p)
 
-    value = loss_sum[:, :rows]
-    for s, copy in enumerate(losses, 1):
-        copy.wait_recv()
-        value = value + loss_in[s]
-    loss_ref[...] = value
-
     for g, result in (("i", gi_ref), ("t", gt_ref)):
         for p in range(PIECES):
             piece = pl.ds(p * part, part)
@@ -304,6 +298,12 @@
             unit_row = values * inverse
             along = jnp.sum(unit_row * grad, axis=-1, keepdims=True)
             result[piece, :] = inverse * (grad - unit_row * along)
+
+    value = loss_sum[:, :rows]
+    for s, copy in enumerate(losses, 1):
+        copy.wait_recv()
+        value = value + loss_in[s]
+    loss_ref[...] = value
 
     for copy in sent:
         copy.wait_send()

time: 34.9 us -> 34.9 us (level)
  no operation moved by 1% of the time
where the time goes in v3:
time: 34.9 us; the launch traced here: 34.8 us
  Pallas kernels  32.8 us (94%)
  between operations  1.93 us (6%)
    pallas_call x1, Pallas kernels, on_device(): pl.pallas_call(functools.partial(kernel, dims), out_shape=(pltpu.VMEM((ro...  32 us
    pallas_call x1, Pallas kernels, on_device(): pl.pallas_call(hand_out, out_shape=(jax.ShapeDtypeStruct((rows, width), f...  0.84 us

profile of v3, /device:TPU:0, one launch (start us, length us, event | category | flops | bytes accessed | tf_op | source)
XLA Modules:
  0.0 34.8 jit_solution(18302131245389936275)
XLA Ops:
  1.9 32.0 %shard_map.67 = (f32[64,1152]{1,0:T(8,128)S(1)}, f32[64,1152]{1,0:T(8,128)S(1)}, f32[1,64]{1,0:T(1,128)S(1)}) custom-call(bf16[64,1152]{1,0:T(8,128)(2,1)} %img_hbm.1, bf16[64,1152]{1,0:T(8,128)(2,1)} %txt_hbm.1, f32[1]{0:T(128)S(6)} %copy.7.scale_ref, f32[1]{0:T(128)S(6)} %copy.8.shift_ref), custom_call_target="tpu_custom_call" | custom-call | tf_op jit(solution)/shard_map/pallas_call | solution.py:329
  33.9 0.8 %shard_map.68 = (f32[64,1152]{1,0:T(8,128)}, f32[64,1152]{1,0:T(8,128)}, f32[1,64]{1,0:T(1,128)}) custom-call(f32[64,1152]{1,0:T(8,128)S(1)} %get-tuple-element.9.gi_from, f32[64,1152]{1,0:T(8,128)S(1)} %get-tuple-element.10.gt_from, f32[1,64]{1,0:T(1,128)S(1)} %get-tuple-element.11.loss_from), custom_call_target="tpu_custom_call" | custom-call | tf_op jit(solution)/shard_map/pallas_call | solution.py:361
